TPU v7x, 32 devices: a whole 2x2x4 slice. The times are simulated.
32 devices in a mesh: group: 2 (over y), ctx: 4 (over z), head: 4 (over x, core).
Axes of the slice: x: 2, y: 2, z: 4, core: 2. Of those that a mesh axis runs over, the one named last changes fastest.
Arguments:
- query_nope: bfloat16 [512, 8192], P(('group', 'ctx'), 'head'), parts along dimension 0, may hold values from -6 to 6
- query_rope: bfloat16 [512, 4096], P(('group', 'ctx'), 'head'), parts along dimension 0, may hold values from -16 to 16
- kv_latent: bfloat16 [512, 512], P(('group', 'ctx'), 'head'), parts along dimension 0, may hold values from -1300 to 1300
- key_rope: bfloat16 [512, 64], P(('group', 'ctx')), parts along dimension 0, may hold values from -16 to 16
- latent_gain: float32 [512], replicated, may hold values from 0.1 to 1.9
- w_key: bfloat16 [512, 8192], P(None, 'head'), may hold values from -0.25 to 0.25
- w_value: bfloat16 [512, 8192], P(None, 'head'), may hold values from -0.25 to 0.25
- block_order: int32 [16], P('group'), parts along dimension 0, may hold values from 0 to 7, as said below
Outputs:
- attention_out: bfloat16 [512, 8192], P(('group', 'ctx'), 'head'), parts along dimension 0
There are 2 independent parts, one for each index of `group`. A program takes and returns all parts, laid end to end along the dimension named above; an argument that names none is the same for every part. Nothing has to cross between parts.
Inputs may be any that keep to these rules, and one draw needn't show every extreme that they name: `block_order`: A permutation of 0 to 7. Entries 2 c and 2 c + 1, for each c < 4, add up to 7.
All inputs are finite; a program needn't handle non-finite values.
Results may differ from a plain program's by a relative error of at most 0.0081.
Values may be sent and summed in bfloat16 or wider, within the bound.
A program may use at most 64 MiB of HBM per device.

v0:
```python
from functools import partial
import math
import jax
import jax.numpy as jnp
from jax import lax
from jax.sharding import PartitionSpec as P

ROPE = 64
NOPE = 128
VALUE_DIM = 128
EPSILON = 1e-06
NEGATIVE = -1e30


def rope_angle(positions, width):
    half_width = width // 2
    frequency = jnp.exp(-jnp.log(10000.0) * jnp.arange(half_width, dtype=jnp.float32) / half_width)
    return positions.astype(jnp.float32)[:, None] * frequency[None, :]


def rotate_pairs(values, angle):
    half_width = values.shape[-1] // 2
    first_half = values[..., :half_width]
    second = values[..., half_width:]
    cosine = jnp.cos(angle)
    sine_part = jnp.sin(angle)
    return jnp.concatenate(
        [first_half * cosine - second * sine_part, second * cosine + first_half * sine_part], -1
    )


def block_positions(begin_row, row_count, table, block_rows):
    row_ids = begin_row + jnp.arange(row_count, dtype=jnp.int32)
    blocks = row_ids // block_rows
    slot_ids = jnp.arange(table.shape[0], dtype=jnp.int32)
    looked = jnp.sum(jnp.where(blocks[:, None] == slot_ids[None, :], table[None, :], 0), axis=1)
    return looked * block_rows + row_ids % block_rows


def block_length(row_count, shard_rows):
    best_rows = shard_rows
    for factor in range(1, row_count // shard_rows + 1):
        if row_count // shard_rows % factor == 0 and shard_rows * factor <= max(512, shard_rows):
            best_rows = shard_rows * factor
    return best_rows


def attend_block(
    carried,
    query_latent,
    query_rotated,
    query_place,
    key_latent,
    key_rotated,
    key_place,
    score_scale,
):
    running_max, running_total, summed = carried
    contract = (((1,), (1,)), ((), ()))
    scores = lax.dot_general(query_latent, key_latent, contract, preferred_element_type=jnp.float32)
    scores = (
        scores
        + lax.dot_general(query_rotated, key_rotated, contract, preferred_element_type=jnp.float32)
    ) * score_scale
    visible = key_place[None, :] <= query_place[:, None]
    scores = jnp.where(visible, scores, NEGATIVE)
    new_max = jnp.maximum(running_max, jnp.max(scores, axis=1))
    exps = jnp.where(visible, jnp.exp(scores - new_max[:, None]), 0.0)
    shrink = jnp.exp(running_max - new_max)
    running_total = running_total * shrink + jnp.sum(exps, axis=1)
    summed = summed * shrink[:, None] + jnp.dot(
        exps.astype(jnp.bfloat16), key_latent, preferred_element_type=jnp.float32
    )
    return (new_max, running_total, summed)


def per_device(
    query_nope, query_rope, kv_latent, key_rope, latent_gain, w_key, w_value, block_order
):
    tokens_here = query_nope.shape[0]
    heads_here = w_key.shape[1] // NOPE
    latent_width = w_key.shape[0]
    block_rows = tokens_here // 2
    score_scale = 1.0 / math.sqrt(NOPE + ROPE)
    first_row = lax.axis_index("ctx") * tokens_here
    query_place = block_positions(first_row, tokens_here, block_order, block_rows)
    query_angle = rope_angle(query_place, ROPE)
    query_rotated = rotate_pairs(
        query_rope.astype(jnp.float32).reshape(tokens_here, heads_here, ROPE),
        query_angle[:, None, :],
    )
    query_rotated = query_rotated.astype(jnp.bfloat16).reshape(tokens_here * heads_here, ROPE)
    absorbed = jnp.einsum(
        "thd,lhd->thl",
        query_nope.reshape(tokens_here, heads_here, NOPE),
        w_key.reshape(latent_width, heads_here, NOPE),
        preferred_element_type=jnp.float32,
    )
    absorbed = absorbed.astype(jnp.bfloat16).reshape(tokens_here * heads_here, latent_width)
    row_place = jnp.repeat(query_place, heads_here)
    groups = ((absorbed, query_rotated, row_place),)
    initial = tuple(
        (
            (
                jnp.full((member[0].shape[0],), NEGATIVE, jnp.float32),
                jnp.zeros((member[0].shape[0],), jnp.float32),
                jnp.zeros((member[0].shape[0], latent_width), jnp.float32),
            )
            for member in groups
        )
    )
    columns = kv_latent.shape[1]
    column_part = kv_latent.astype(jnp.float32)
    square = lax.psum(jnp.sum(column_part * column_part, axis=1), "head")
    gain_part = lax.dynamic_slice_in_dim(latent_gain, lax.axis_index("head") * columns, columns, 0)
    scaled = (
        column_part * lax.rsqrt(square / latent_width + EPSILON)[:, None] * gain_part[None, :]
    ).astype(jnp.bfloat16)
    normed = lax.all_gather(scaled, "head", axis=1, tiled=True)
    key_rotated = rotate_pairs(key_rope.astype(jnp.float32), query_angle).astype(jnp.bfloat16)
    key_latent = lax.all_gather(normed, "ctx", axis=0, tiled=True)
    make_key_rotated = lax.all_gather(key_rotated, "ctx", axis=0, tiled=True)
    row_count = key_latent.shape[0]
    length = block_length(row_count, tokens_here)
    block_count = row_count // length
    latent_blocks = key_latent.reshape(block_count, length, latent_width)
    rotated_blocks = make_key_rotated.reshape(block_count, length, ROPE)
    block_starts = length * jnp.arange(block_count, dtype=jnp.int32)

    def one_block(state_now, operands):
        latent_block, rotated_block, first_key = operands
        key_place = block_positions(first_key, length, block_order, block_rows)
        updated = []
        for member, member_state in zip(groups, state_now):
            advance = partial(
                attend_block,
                query_latent=member[0],
                query_rotated=member[1],
                query_place=member[2],
                key_latent=latent_block,
                key_rotated=rotated_block,
                key_place=key_place,
                score_scale=score_scale,
            )
            updated.append(advance(member_state))
        return (tuple(updated), None)

    result, unused = lax.scan(one_block, initial, (latent_blocks, rotated_blocks, block_starts))
    mixed = jnp.concatenate(
        [
            (member_state[2] / member_state[1][:, None]).astype(jnp.bfloat16)
            for member_state in result
        ],
        0,
    )
    mixed = mixed.reshape(tokens_here, heads_here, latent_width)
    output = jnp.einsum(
        "thl,lhe->the",
        mixed,
        w_value.reshape(latent_width, heads_here, VALUE_DIM),
        preferred_element_type=jnp.float32,
    )
    return output.astype(jnp.bfloat16).reshape(tokens_here, heads_here * VALUE_DIM)


def solution(mesh):
    return jax.shard_map(
        per_device,
        mesh=mesh,
        in_specs=(
            P(("group", "ctx"), "head"),
            P(("group", "ctx"), "head"),
            P(("group", "ctx"), "head"),
            P(("group", "ctx"), None),
            P(),
            P(None, "head"),
            P(None, "head"),
            P("group"),
        ),
        out_specs=P(("group", "ctx"), "head"),
        check_vma=False,
    )
```

profile of v0, /device:TPU:0, one launch (start us, length us, event | category | flops | bytes accessed | tf_op | source)
XLA Modules:
  0.0 54.3 jit_solution(1356977436039085521)
XLA Ops:
  0.0 0.0 copy-start
  0.0 0.9 %dynamic_slice.12 = f32[128]{0:T(128)S(1)} dynamic-slice(f32[512]{0:T(512)} %param.12, s32[]{:T(128)S(6)} %select_n.69), dynamic_slice_sizes={128} | dynamic-slice | bytes 1028 | tf_op jit(solution)/shard_map/dynamic_slice | solution.py:115
  0.9 0.8 %fusion.33 = f32[64]{0:T(128)S(1)} fusion(bf16[64,128]{1,0:T(8,128)(2,1)} %param.10), kind=kLoop, calls=%fused_computation.34 | loop fusion | flops 24512 | bytes 16640 | tf_op jit(solution)/shard_map/reduce_sum | solution.py:114
  1.7 8.4 %psum.7 = f32[64]{0:T(128)S(1)} all-reduce(f32[64]{0:T(128)S(1)} %fusion.33), channel_id=1, replica_groups=mesh['group'=2,'ctx'=4,'head'=4] {'head'}, use_global_device_ids=true, to_apply=%region_3.4 | all-reduce | flops 64 | bytes 512 | tf_op jit(solution)/shard_map/psum | solution.py:114
  10.1 0.8 %fusion.35 = bf16[64,128]{1,0:T(8,128)(2,1)S(1)} fusion(bf16[64,128]{1,0:T(8,128)(2,1)} %param.10, f32[128]{0:T(128)S(1)} %dynamic_slice.12, f32[64]{0:T(128)S(1)} %add_rsqrt_fusion), kind=kLoop, calls=%fused_computation.36 | loop fusion | flops 32768 | bytes 33536 | tf_op jit(solution)/shard_map/convert_element_type | solution.py:118
  10.9 5.3 %all_gather.9 = bf16[64,512]{1,0:T(8,128)(2,1)S(1)} all-gather(bf16[64,128]{1,0:T(8,128)(2,1)S(1)} %fusion.35), channel_id=1, replica_groups=mesh['group'=2,'ctx'=4,'head'=4] {'head'}, dimensions={1}, use_global_device_ids=true | all-gather | bytes 81920 | tf_op jit(solution)/shard_map/all_gather | solution.py:119
  16.2 14.1 %all_gather.10 = bf16[256,512]{1,0:T(8,128)(2,1)S(1)} all-gather(bf16[64,512]{1,0:T(8,128)(2,1)S(1)} %all_gather.9), channel_id=1, replica_groups=mesh['group'=2,'ctx'=4,'head'=4] {'ctx'}, dimensions={0}, use_global_device_ids=true | all-gather | bytes 327680 | tf_op jit(solution)/shard_map/all_gather | solution.py:121
  30.2 0.0 copy-done
  30.2 1.8 %fusion.9 = bf16[64,16,512]{2,0,1:T(8,128)(2,1)S(1)} fusion(bf16[512,2048]{1,0:T(8,128)(2,1)S(1)} %copy-done, bf16[64,2048]{1,0:T(8,128)(2,1)} %param.8), kind=kOutput, calls=%fused_computation.8 | convolution fusion | flops 134742016 | bytes 3407872 | tf_op jit(solution)/shard_map/thd,lhd->thl/dot_general | solution.py:93
  32.0 0.0 copy-start.3
  32.1 0.0 copy-start.2
  32.1 0.0 copy-start.1
  32.1 0.6 %copy.21 = bf16[64,16,512]{2,1,0:T(8,128)(2,1)S(1)} copy(bf16[64,16,512]{2,0,1:T(8,128)(2,1)S(1)} %fusion.9) | data formatting | bytes 2097152 | tf_op jit(solution)/shard_map/convert_element_type | solution.py:99
  32.7 1.5 %fusion.46 = f32[1024,256]{0,1:T(8,128)} fusion(bf16[1024,512]{1,0:T(8,128)(2,1)S(1)} %bitcast.45, bf16[256,512]{1,0:T(8,128)(2,1)S(1)} %all_gather.10), kind=kOutput, calls=%fused_computation.68 | convolution fusion | flops 268435456 | bytes 2359296 | tf_op jit(solution)/shard_map/while/body/eval_jaxpr/dot_general | solution.py:60
  34.1 0.0 copy-done.3
  34.2 0.1 select_reduce_fusion.1
  34.3 0.0 copy-done.2
  34.3 0.2 multiply_cosine_fusion
  34.5 0.1 pad_maximum_fusion
  34.6 13.3 %all_gather.11 = bf16[256,64]{1,0:T(8,128)(2,1)S(1)} all-gather(bf16[64,64]{1,0:T(8,128)(2,1)S(1)} %pad_maximum_fusion), channel_id=1, replica_groups=mesh['group'=2,'ctx'=4,'head'=4] {'ctx'}, dimensions={0}, use_global_device_ids=true | all-gather | bytes 40960 | tf_op jit(solution)/shard_map/all_gather | solution.py:122
  47.9 0.0 copy-done.1
  47.9 0.1 reshape.178
  48.0 0.2 subtract_convert_fusion
  48.2 0.1 broadcast_in_dim.74
  48.3 0.1 le.23
  48.4 0.1 select_reduce_fusion
  48.5 1.7 %fusion.45 = (f32[1024]{0:T(1024)S(1)}, f32[1024,256]{0,1:T(8,128)S(1)}) fusion(f32[1024,256]{0,1:T(8,128)} %fusion.46, bf16[256,64]{1,0:T(8,128)(2,1)S(1)} %all_gather.11, bf16[1024,32]{1,0:T(8,128)(2,1)S(1)} %bitcast.47, bf16[1024,32]{1,0:T(8,128)(2,1)S(1)} %bitcast.46, s32[1024]{0:T(1024)S(1)} %le.23, s32[256]{0:T(256)S(1)} %fusion.38), kind=kOutput, calls=%fused_computation.67 | convolution fusion | flops 35126272 | bytes 2270208 | tf_op jit(solution)/shard_map/while/body/eval_jaxpr/dot_general | solution.py:63
  50.2 0.2 fusion.21
  50.4 0.0 copy-start.4
  50.4 0.6 %divide_convert_fusion = bf16[1024,512]{1,0:T(8,128)(2,1)S(1)} fusion(bf16[256,512]{1,0:T(8,128)(2,1)S(1)} %all_gather.10, f32[1024]{0:T(1024)S(1)} %get-tuple-element.40, f32[1024]{0:T(1024)S(1)} %get-tuple-element.29, f32[1024,256]{0,1:T(8,128)S(1)} %get-tuple-element.48, f32[1024]{0:T(1024)S(1)} %broadcast_maximum_fusion, s32[1024]{0:T(1024)S(1)} %le.23, ...), kind=kOutput, calls=%fused_computation.6 | convolution fusion | flops 271056896 | bytes 2376704 | tf_op jit(solution)/shard_map/while/body/eval_jaxpr/dot_general | solution.py:71
  51.0 1.0 %copy-done.4 = bf16[512,2048]{1,0:T(8,128)(2,1)S(1)} copy-done((bf16[512,2048]{1,0:T(8,128)(2,1)S(1)}, bf16[512,2048]{1,0:T(8,128)(2,1)}, u32[]{:S(2)}) %copy-start.4) | copy-done | bytes 2097176
  52.0 1.5 %fusion.17 = bf16[16,8,8,128]{3,2,1,0:T(8,128)(2,1)S(1)} fusion(bf16[64,16,512]{2,1,0:T(8,128)(2,1)S(1)} %bitcast.48, bf16[512,2048]{1,0:T(8,128)(2,1)S(1)} %copy-done.4), kind=kOutput, calls=%fused_computation.14 | convolution fusion | flops 134348800 | bytes 3407872 | tf_op jit(solution)/shard_map/thl,lhe->the/dot_general | solution.py:157
  53.5 0.8 %copy.52 = bf16[16,8,8,128]{3,2,0,1:T(8,128)(2,1)} copy(bf16[16,8,8,128]{3,2,1,0:T(8,128)(2,1)S(1)} %fusion.17) | data formatting | bytes 524288 | tf_op jit(solution)/shard_map/reshape | solution.py:163
  (9 shorter events, 0.1 us)
Async XLA Ops:
  0.0 30.2 %copy-start = (bf16[512,2048]{1,0:T(8,128)(2,1)S(1)}, bf16[512,2048]{1,0:T(8,128)(2,1)}, u32[]{:S(2)}) copy-start(bf16[512,2048]{1,0:T(8,128)(2,1)} %param.13) | copy-start | bytes 6291460
  32.0 2.1 %copy-start.3 = (s32[8]{0:T(128)S(1)}, s32[8]{0:T(128)}, u32[]{:S(2)}) copy-start(s32[8]{0:T(128)} %param.15) | copy-start | bytes 100
  32.1 2.2 %copy-start.2 = (bf16[64,64]{1,0:T(8,128)(2,1)S(1)}, bf16[64,64]{1,0:T(8,128)(2,1)}, u32[]{:S(2)}) copy-start(bf16[64,64]{1,0:T(8,128)(2,1)} %param.11) | copy-start | bytes 24580
  32.1 15.8 %copy-start.1 = (bf16[64,1024]{1,0:T(8,128)(2,1)S(1)}, bf16[64,1024]{1,0:T(8,128)(2,1)}, u32[]{:S(2)}) copy-start(bf16[64,1024]{1,0:T(8,128)(2,1)} %param.9) | copy-start | bytes 393220
  50.4 1.6 %copy-start.4 = (bf16[512,2048]{1,0:T(8,128)(2,1)S(1)}, bf16[512,2048]{1,0:T(8,128)(2,1)}, u32[]{:S(2)}) copy-start(bf16[512,2048]{1,0:T(8,128)(2,1)} %param.14) | copy-start | bytes 6291460
where the time goes:
time: 54.7 us; the launch traced here: 54.3 us
  blocking collectives  41 us (75%)
  matrix products  7 us (13%)
  local copies, waits for them, and re-layouts  3.53 us (6%)
  other arithmetic  2.6 us (5%)
    all_gather x1, blocking collectives, per_device(): key_latent = lax.all_gather(normed, 'ctx', axis=0, tiled=True)  14.1 us
    all_gather x1, blocking collectives, per_device(): make_key_rotated = lax.all_gather(key_rotated, 'ctx', axis=0, tiled=True)  13.3 us
    psum x1, blocking collectives, per_device(): square = lax.psum(jnp.sum(column_part * column_part, axis=1), 'head')  8.37 us
    all_gather x1, blocking collectives, per_device(): normed = lax.all_gather(scaled, 'head', axis=1, tiled=True)  5.25 us
    dot_general x1, matrix products, per_device(): jnp.einsum('thd,lhd->thl', query_nope.reshape(tokens_here, heads_here, NO...  1.79 us
    dot_general x1, matrix products, attend_block(): lax.dot_general(query_rotated, key_rotated, contract, preferred_element_t...  1.65 us
    dot_general x1, matrix products, per_device(): jnp.einsum('thl,lhe->the', mixed, w_value.reshape(latent_width, heads_her...  1.49 us
    dot_general x1, matrix products, attend_block(): lax.dot_general(query_latent, key_latent, contract, preferred_element_typ...  1.46 us

commit v1 on v0

--- a/solution.py
+++ b/solution.py
@@ -119,7 +119,9 @@
     normed = lax.all_gather(scaled, "head", axis=1, tiled=True)
     key_rotated = rotate_pairs(key_rope.astype(jnp.float32), query_angle).astype(jnp.bfloat16)
     key_latent = lax.all_gather(normed, "ctx", axis=0, tiled=True)
-    make_key_rotated = lax.all_gather(key_rotated, "ctx", axis=0, tiled=True)
+    make_key_rotated = jnp.concatenate(
+        lax.all_to_all(jnp.stack([key_rotated] * lax.axis_size("ctx")), "ctx", 0, 0), axis=0
+    )
     row_count = key_latent.shape[0]
     length = block_length(row_count, tokens_here)
     block_count = row_count // length

time: 54.7 us -> 50.5 us (0.923)
  blocking collectives: 41 us -> 25.8 us
  starting transfers between devices: 0 us -> 6.35 us
  local copies, waits for them, and re-layouts: 3.53 us -> 5.23 us
  other arithmetic: 2.6 us -> 4.1 us
  matrix products: 7 us -> 8.3 us
    all_gather x1 -> x0, blocking collectives: 13.3 us -> none  [per_device(): make_key_rotated = lax.all_gather(key_rotated, 'ctx', axis=0, tiled=True)]
    all_to_all x0 -> x1, starting transfers between devices: none -> 6.35 us  [per_device(): lax.all_to_all(jnp.stack([key_rotated] * lax.axis_size('ctx')), 'ctx', 0, 0)]
    psum x1, blocking collectives: 8.37 us -> 6.6 us  [per_device(): square = lax.psum(jnp.sum(column_part * column_part, axis=1), 'head')]
    dot_general x1, matrix products: 1.46 us -> 2.73 us  [attend_block(): lax.dot_general(query_latent, key_latent, contract, preferred_element_typ...]
    convert_element_type x1, local copies, waits for them, and re-layouts: 0.58 us -> 1.57 us  [per_device(): absorbed.astype(jnp.bfloat16)]
    unnamed x10, local copies, waits for them, and re-layouts: 1 us -> 1.84 us
    reduce_sum x2, other arithmetic: 0.17 us -> 0.97 us  [block_positions(): jnp.sum(jnp.where(blocks[:, None] == slot_ids[None, :], table[None, :], 0...]
    convert_element_type x1, other arithmetic: 0.01 us -> 0.72 us  [per_device(): key_rope.astype(jnp.float32)]
  transfers between devices with their start and end apart: 0 -> 1, of which waited for: 0 -> 0; matrix products, arithmetic and copies ran while one was open for 0% -> 18% of each run, Pallas kernels for 0% -> 0%
where the time goes in v1:
time: 50.5 us; the launch traced here: 49.9 us
  blocking collectives  25.8 us (51%)
  matrix products  8.3 us (16%)
  starting transfers between devices  6.35 us (13%)
  local copies, waits for them, and re-layouts  5.23 us (10%)
  other arithmetic  4.1 us (8%)
    all_gather x1, blocking collectives, per_device(): key_latent = lax.all_gather(normed, 'ctx', axis=0, tiled=True)  14 us
    psum x1, blocking collectives, per_device(): square = lax.psum(jnp.sum(column_part * column_part, axis=1), 'head')  6.6 us
    all_to_all x1, starting transfers between devices, per_device(): lax.all_to_all(jnp.stack([key_rotated] * lax.axis_size('ctx')), 'ctx', 0, 0)  6.35 us
    all_gather x1, blocking collectives, per_device(): normed = lax.all_gather(scaled, 'head', axis=1, tiled=True)  5.25 us
    dot_general x1, matrix products, attend_block(): lax.dot_general(query_latent, key_latent, contract, preferred_element_typ...  2.73 us
    unnamed x10, local copies, waits for them, and re-layouts  1.84 us
    dot_general x1, matrix products, per_device(): jnp.einsum('thd,lhd->thl', query_nope.reshape(tokens_here, heads_here, NO...  1.83 us
    dot_general x1, matrix products, attend_block(): lax.dot_general(query_rotated, key_rotated, contract, preferred_element_t...  1.65 us
  transfers between devices with their start and end apart: 1, of which 0 were waited for; matrix products, arithmetic and copies ran while one was open for 18% of the time, Pallas kernels for 0%

profile of v1, /device:TPU:0, one launch (start us, length us, event | category | flops | bytes accessed | tf_op | source)
XLA Modules:
  0.0 49.9 jit_solution(5494451421850506144)
XLA Ops:
  0.0 0.0 copy-start
  0.0 0.9 %select_reduce_fusion.1 = s32[64]{0:T(128)S(1)} fusion(s32[8]{0:T(128)} %param.15, s32[64]{0:T(128)S(1)} %and_select_fusion.1), kind=kLoop, calls=%fused_computation.43 | loop fusion | flops 1472 | bytes 544 | tf_op jit(solution)/shard_map/reduce_sum | solution.py:36
  0.9 0.7 %convert_element_type.46 = f32[64,64]{1,0:T(8,128)S(1)} convert(bf16[64,64]{1,0:T(8,128)(2,1)} %param.11) | non-fusion elementwise | flops 4096 | bytes 24576 | tf_op jit(solution)/shard_map/convert_element_type | solution.py:120
  1.7 0.2 multiply_cosine_fusion
  1.9 0.1 pad_maximum_fusion
  1.9 0.7 %reshape.184 = bf16[4,2,2048]{2,1,0:T(2,128)(2,1)} reshape(bf16[4,64,64]{2,1,0:T(8,128)(2,1)S(1)} %stack.2) | data formatting | bytes 65536
  2.7 6.3 %all-to-all-start = ((bf16[4,2,2048]{2,1,0:T(2,128)(2,1)}), bf16[4,2,2048]{2,1,0:T(2,128)(2,1)S(1)}, u32[]{:S(2)}, u32[]{:S(2)}) async-start(bf16[4,2,2048]{2,1,0:T(2,128)(2,1)} %reshape.184), calls=%async_computation | async-start | bytes 65536 | tf_op jit(solution)/shard_map/all_to_all | solution.py:123
  9.0 0.8 %fusion.33 = f32[64]{0:T(128)S(1)} fusion(bf16[64,128]{1,0:T(8,128)(2,1)} %param.10), kind=kLoop, calls=%fused_computation.34 | loop fusion | flops 24512 | bytes 16640 | tf_op jit(solution)/shard_map/reduce_sum | solution.py:114
  9.9 6.6 %psum.7 = f32[64]{0:T(128)S(1)} all-reduce(f32[64]{0:T(128)S(1)} %fusion.33), channel_id=1, replica_groups=mesh['group'=2,'ctx'=4,'head'=4] {'head'}, use_global_device_ids=true, to_apply=%region_3.4 | all-reduce | flops 64 | bytes 512 | tf_op jit(solution)/shard_map/psum | solution.py:114
  16.5 0.8 %dynamic_slice.12 = f32[128]{0:T(128)S(1)} dynamic-slice(f32[512]{0:T(512)} %param.12, s32[]{:T(128)S(6)} %select_n.69), dynamic_slice_sizes={128} | dynamic-slice | bytes 1028 | tf_op jit(solution)/shard_map/dynamic_slice | solution.py:115
  17.2 0.8 %fusion.35 = bf16[64,128]{1,0:T(8,128)(2,1)S(1)} fusion(bf16[64,128]{1,0:T(8,128)(2,1)} %param.10, f32[128]{0:T(128)S(1)} %dynamic_slice.12, f32[64]{0:T(128)S(1)} %add_rsqrt_fusion), kind=kLoop, calls=%fused_computation.36 | loop fusion | flops 32768 | bytes 33536 | tf_op jit(solution)/shard_map/convert_element_type | solution.py:118
  18.0 5.3 %all_gather.6 = bf16[64,512]{1,0:T(8,128)(2,1)S(1)} all-gather(bf16[64,128]{1,0:T(8,128)(2,1)S(1)} %fusion.35), channel_id=1, replica_groups=mesh['group'=2,'ctx'=4,'head'=4] {'head'}, dimensions={1}, use_global_device_ids=true | all-gather | bytes 81920 | tf_op jit(solution)/shard_map/all_gather | solution.py:119
  23.3 14.0 %all_gather.7 = bf16[256,512]{1,0:T(8,128)(2,1)S(1)} all-gather(bf16[64,512]{1,0:T(8,128)(2,1)S(1)} %all_gather.6), channel_id=1, replica_groups=mesh['group'=2,'ctx'=4,'head'=4] {'ctx'}, dimensions={0}, use_global_device_ids=true | all-gather | bytes 327680 | tf_op jit(solution)/shard_map/all_gather | solution.py:121
  37.2 0.0 copy-done
  37.2 0.0 copy-start.1
  37.2 1.8 %fusion.9 = bf16[64,16,512]{2,0,1:T(8,128)(2,1)S(1)} fusion(bf16[512,2048]{1,0:T(8,128)(2,1)S(1)} %copy-done, bf16[64,2048]{1,0:T(8,128)(2,1)} %param.8), kind=kOutput, calls=%fused_computation.8 | convolution fusion | flops 134742016 | bytes 3407872 | tf_op jit(solution)/shard_map/thd,lhd->thl/dot_general | solution.py:93
  39.1 0.0 copy-start.2
  39.1 1.6 %copy.21 = bf16[64,16,512]{2,1,0:T(8,128)(2,1)} copy(bf16[64,16,512]{2,0,1:T(8,128)(2,1)S(1)} %fusion.9) | data formatting | bytes 2097152 | tf_op jit(solution)/shard_map/convert_element_type | solution.py:99
  40.7 0.0 copy-done.1
  40.7 0.1 reshape.183
  40.8 0.0 copy-done.2
  40.8 0.1 select_reduce_fusion
  40.9 2.7 %fusion.46 = f32[1024,256]{0,1:T(8,128)} fusion(bf16[1024,512]{1,0:T(8,128)(2,1)} %bitcast.46, bf16[256,512]{1,0:T(8,128)(2,1)S(1)} %all_gather.7), kind=kOutput, calls=%fused_computation.68 | convolution fusion | flops 268435456 | bytes 2359296 | tf_op jit(solution)/shard_map/while/body/eval_jaxpr/dot_general | solution.py:60
  43.6 0.2 subtract_convert_fusion
  43.9 0.1 broadcast_in_dim.74
  43.9 0.1 le.23
  44.0 0.0 all-to-all-done
  44.0 0.1 reshape.185
  44.2 1.6 %fusion.45 = (f32[1024]{0:T(1024)S(1)}, f32[1024,256]{0,1:T(8,128)S(1)}) fusion(f32[1024,256]{0,1:T(8,128)} %fusion.46, bf16[256,64]{1,0:T(8,128)(2,1)S(1)} %bitcast.49, bf16[1024,32]{1,0:T(8,128)(2,1)S(1)} %bitcast.48, bf16[1024,32]{1,0:T(8,128)(2,1)S(1)} %bitcast.47, s32[1024]{0:T(1024)S(1)} %le.23, s32[256]{0:T(256)S(1)} %fusion.38), kind=kOutput, calls=%fused_computation.67 | convolution fusion | flops 35126272 | bytes 2270208 | tf_op jit(solution)/shard_map/while/body/eval_jaxpr/dot_general | solution.py:63
  45.8 0.2 fusion.21
  46.1 0.0 copy-start.3
  46.1 0.6 %divide_convert_fusion = bf16[1024,512]{1,0:T(8,128)(2,1)S(1)} fusion(bf16[256,512]{1,0:T(8,128)(2,1)S(1)} %all_gather.7, f32[1024]{0:T(1024)S(1)} %get-tuple-element.40, f32[1024]{0:T(1024)S(1)} %get-tuple-element.29, f32[1024,256]{0,1:T(8,128)S(1)} %get-tuple-element.48, f32[1024]{0:T(1024)S(1)} %broadcast_maximum_fusion, s32[1024]{0:T(1024)S(1)} %le.23, ...), kind=kOutput, calls=%fused_computation.6 | convolution fusion | flops 271056896 | bytes 2376704 | tf_op jit(solution)/shard_map/while/body/eval_jaxpr/dot_general | solution.py:71
  46.7 1.0 %copy-done.3 = bf16[512,2048]{1,0:T(8,128)(2,1)S(1)} copy-done((bf16[512,2048]{1,0:T(8,128)(2,1)S(1)}, bf16[512,2048]{1,0:T(8,128)(2,1)}, u32[]{:S(2)}) %copy-start.3) | copy-done | bytes 2097176
  47.7 1.5 %fusion.17 = bf16[16,8,8,128]{3,2,1,0:T(8,128)(2,1)S(1)} fusion(bf16[64,16,512]{2,1,0:T(8,128)(2,1)S(1)} %bitcast.50, bf16[512,2048]{1,0:T(8,128)(2,1)S(1)} %copy-done.3), kind=kOutput, calls=%fused_computation.14 | convolution fusion | flops 134348800 | bytes 3407872 | tf_op jit(solution)/shard_map/thl,lhe->the/dot_general | solution.py:159
  49.2 0.8 %copy.52 = bf16[16,8,8,128]{3,2,0,1:T(8,128)(2,1)} copy(bf16[16,8,8,128]{3,2,1,0:T(8,128)(2,1)S(1)} %fusion.17) | data formatting | bytes 524288 | tf_op jit(solution)/shard_map/reshape | solution.py:165
  (9 shorter events, 0.1 us)
Async XLA Ops:
  0.0 37.2 %copy-start = (bf16[512,2048]{1,0:T(8,128)(2,1)S(1)}, bf16[512,2048]{1,0:T(8,128)(2,1)}, u32[]{:S(2)}) copy-start(bf16[512,2048]{1,0:T(8,128)(2,1)} %param.13) | copy-start | bytes 6291460
  2.7 41.3 %all-to-all-start = ((bf16[4,2,2048]{2,1,0:T(2,128)(2,1)}), bf16[4,2,2048]{2,1,0:T(2,128)(2,1)S(1)}, u32[]{:S(2)}, u32[]{:S(2)}) async-start(bf16[4,2,2048]{2,1,0:T(2,128)(2,1)} %reshape.184), calls=%async_computation | async-start | bytes 65536 | tf_op jit(solution)/shard_map/all_to_all | solution.py:123
  37.2 3.4 %copy-start.1 = (bf16[64,1024]{1,0:T(8,128)(2,1)S(1)}, bf16[64,1024]{1,0:T(8,128)(2,1)}, u32[]{:S(2)}) copy-start(bf16[64,1024]{1,0:T(8,128)(2,1)} %param.9) | copy-start | bytes 393220
  39.1 1.7 %copy-start.2 = (s32[8]{0:T(128)S(1)}, s32[8]{0:T(128)}, u32[]{:S(2)}) copy-start(s32[8]{0:T(128)} %param.15) | copy-start | bytes 100
  46.1 1.6 %copy-start.3 = (bf16[512,2048]{1,0:T(8,128)(2,1)S(1)}, bf16[512,2048]{1,0:T(8,128)(2,1)}, u32[]{:S(2)}) copy-start(bf16[512,2048]{1,0:T(8,128)(2,1)} %param.14) | copy-start | bytes 6291460
